TPU v7x, 256 devices: a whole 4x4x8 slice. The times are simulated.
256 devices in a mesh: rep: 8 (over x, z_lo), blk: 32 (over z_hi, y, core).
Axes of the slice: x: 4, y: 4, z: 8 (z_hi: 4, z_lo: 2; z = z_hi * 2 + z_lo), core: 2. Of those that a mesh axis runs over, the one named last changes fastest.
Arguments:
- positions: float32 [3, 65536], P(None, ('rep', 'blk')), parts along dimension 1, may hold values from 0 to 64
- forces: float32 [6, 3, 65536], P(None, None, ('rep', 'blk')), parts along dimension 2, may hold values from -6 to 6
- random_kicks: float32 [6, 3, 65536], P(None, None, ('rep', 'blk')), parts along dimension 2, may hold values from -4 to 4
- history_velocity: float32 [128, 3, 65536], P(None, None, ('rep', 'blk')), parts along dimension 2, may hold values from -6 to 6
- history_offset: float32 [128, 3, 65536], P(None, None, ('rep', 'blk')), parts along dimension 2, may hold values from -8 to 8
- lag_index: int32 [32768], P(('rep', 'blk')), parts along dimension 0, may hold values from 0 to 127
Outputs:
- final_positions: float32 [3, 65536], P(None, ('rep', 'blk')), parts along dimension 1
- velocity: float32 [3, 65536], P(None, ('rep', 'blk')), parts along dimension 1
- statistics: float32 [2, 32768], P(None, ('rep', 'blk')), parts along dimension 1
There are 8 independent parts, one for each index of `rep`. A program takes and returns all parts, laid end to end along the dimension named above; each array names one. Nothing has to cross between parts.
All inputs are finite; a program needn't handle non-finite values.
Results may differ from a plain program's by a relative error of at most 0.0003.
Values sent between devices are 32-bit elements; how exact they have to be, the bound alone decides.
No kernel may reach another device: no remote copies, remote signals or barrier semaphores. Data moves between devices by JAX's collectives and lax.ppermute only.
A program may use at most 64 MiB of HBM per device.

v0:
```python
import math

import jax
import jax.numpy as jnp
from jax import lax
from jax.sharding import PartitionSpec as P

STEPS = 6


time_step = 0.05


def sent_to_all(x, axis):
    copies = jnp.broadcast_to(x, (lax.axis_size(axis), *x.shape))
    return lax.all_to_all(copies, axis, split_axis=0, concat_axis=0, tiled=True)


def laid_out(parts, dim):
    lengths = list(parts.shape[1:])
    lengths[dim] *= parts.shape[0]
    return jnp.moveaxis(parts, 0, dim).reshape(lengths)


def collect(x, axis, dim):
    parts = sent_to_all(x, axis)
    return laid_out(parts, dim)


def in_one_piece(arrays, axis, dim, along):
    ends, at = ([], 0)
    for a in arrays[:-1]:
        at += a.shape[along]
        ends.append(at)
    both = jnp.concatenate(arrays, axis=along)
    return tuple(jnp.split(collect(both, axis, dim), ends, axis=along))


def over_copies(x, axis):
    everything = sent_to_all(x, axis)
    return jnp.sum(everything, axis=0)


def packed_total(arrays, axis):
    vector, at, finished = (jnp.concatenate([a.reshape(-1) for a in arrays]), 0, [])
    total = over_copies(vector, axis)
    for a in arrays:
        finished.append(total[at : at + a.size].reshape(a.shape))
        at += a.size
    return tuple(finished)


def pair_coefs(targets, sources):
    separation = targets[:, None, :] - sources[:, :, None]
    dist_sq = jnp.sum(separation * separation, axis=0)
    dist_safe = jnp.where(dist_sq > 0.0, dist_sq, 1.0)
    inv_dist = lax.rsqrt(dist_safe)
    distance = dist_sq * inv_dist
    inv_sq = 1.0 / dist_safe
    far_mask = distance >= 2.0
    coef_iso = jnp.where(
        far_mask, 0.75 * inv_dist * (1.0 + 2.0 / 3.0 * inv_sq), 1.0 - 9.0 / 32.0 * distance
    )
    coef_dir = jnp.where(
        far_mask, 0.75 * inv_dist * (1.0 - 2.0 * inv_sq) * inv_sq, 3.0 / 32.0 * inv_dist
    )
    return (separation, coef_iso, coef_dir)


def pair_velocity(targets, sources, loads):
    separation, coef_iso, coef_dir = pair_coefs(targets, sources)
    projection = jnp.sum(separation * loads[:, :, None], axis=0)
    return jnp.sum(
        coef_iso[None] * loads[:, :, None] + (coef_dir * projection)[None] * separation, axis=1
    )


def blockwise(targets, sources, loads):
    source_count = sources.shape[1]
    row_count = math.gcd(source_count, 512)
    block_count = source_count // row_count
    source_blocks = sources.reshape(3, block_count, row_count).transpose(1, 0, 2)
    load_blocks = loads.reshape(3, block_count, row_count).transpose(1, 0, 2)

    def accumulate(running, source_block):
        return (running + pair_velocity(targets, source_block[0], source_block[1]), None)

    running, unused = lax.scan(
        accumulate, jnp.zeros(targets.shape, jnp.float32), (source_blocks, load_blocks)
    )
    return running


def local(positions, forces, random_kicks, history_velocity, history_offset, lag_index):
    places = positions
    velocity = jnp.zeros_like(positions)
    for step_index in range(STEPS):
        targets = places
        own_forces = forces[step_index]
        pieces = in_one_piece((targets, own_forces), "blk", 1, 0)
        velocity = blockwise(targets, pieces[0], pieces[1])
        places = places + time_step * velocity + random_kicks[step_index]
    velocity_dot = jnp.sum(velocity[None] * history_velocity, axis=(1, 2))
    moved = places[None] - positions[None] - history_offset
    square_disp = jnp.sum(moved * moved, axis=(1, 2))
    frames = history_velocity.shape[0]
    sphere_total = jnp.float32(positions.shape[1] * lax.axis_size("blk"))
    vdot_sum, disp_sum = packed_total((velocity_dot, square_disp), "blk")
    onehot = (lag_index[:, None] == jnp.arange(frames, dtype=jnp.int32)[None, :]).astype(
        jnp.float32
    )
    frame_table = jnp.stack([vdot_sum, disp_sum], axis=1)
    picked = jnp.dot(
        onehot, frame_table, precision=lax.Precision.HIGHEST, preferred_element_type=jnp.float32
    )
    statistics = picked.T / sphere_total
    return (places, velocity, statistics)


def solution(mesh):
    return jax.shard_map(
        local,
        mesh=mesh,
        in_specs=(
            P(None, ("rep", "blk")),
            P(None, None, ("rep", "blk")),
            P(None, None, ("rep", "blk")),
            P(None, None, ("rep", "blk")),
            P(None, None, ("rep", "blk")),
            P(("rep", "blk")),
        ),
        out_specs=(P(None, ("rep", "blk")), P(None, ("rep", "blk")), P(None, ("rep", "blk"))),
        check_vma=False,
    )
```

profile of v0, /device:TPU:1, one launch (start us, length us, event | category | flops | bytes accessed | tf_op | source)
XLA Modules:
  0.0 268.5 jit_solution(17276882879470259727)
XLA Ops:
  0.6 0.8 slice_bitcast_fusion
  1.4 0.7 pad_maximum_fusion
  2.1 0.7 broadcast_in_dim.57
  2.8 12.9 %all-to-all-start = ((f32[32,6,256]{2,1,0:T(8,128)}), f32[32,6,256]{2,1,0:T(8,128)S(1)}, u32[]{:S(2)}, u32[]{:S(2)}) async-start(f32[32,6,256]{2,1,0:T(8,128)} %broadcast_in_dim.57), calls=%async_computation | async-start | bytes 524288 | tf_op jit(solution)/shard_map/all_to_all | solution.py:16
  15.7 13.4 %all-to-all-done = f32[32,6,256]{2,1,0:T(8,128)S(1)} async-done(((f32[32,6,256]{2,1,0:T(8,128)}), f32[32,6,256]{2,1,0:T(8,128)S(1)}, u32[]{:S(2)}, u32[]{:S(2)}) %all-to-all-start) | async-done | bytes 196640 | tf_op jit(solution)/shard_map/all_to_all | solution.py:16
  29.1 22.4 %while.66 = (s32[]{:T(128)}, f32[3,256]{1,0:T(4,128)S(1)}, f32[3,256]{1,0:T(4,128)S(1)}, f32[16,3,512]{2,1,0:T(4,128)S(1)}, f32[16,3,512]{2,1,0:T(4,128)S(1)}, /*index=5*/s32[]{:T(128)}, s32[]{:T(128)}) while((s32[]{:T(128)}, f32[3,256]{1,0:T(4,128)S(1)}, f32[3,256]{1,0:T(4,128)S(1)}, f32[16,3,512]{2,1,0:T(4,128)S(1)}, ...), condition=%wide.region_4.5_spmd.clone, body=%wide.region_0.4_spmd.clone.sunk | while | flops 6161155 | bytes 4261979 | solution.py:88
  30.0 0.5 fusion.73
  31.4 0.5 fusion.73
  32.8 0.5 fusion.73
  34.2 0.5 fusion.73
  35.6 0.5 fusion.73
  37.0 0.5 fusion.73
  38.4 0.5 fusion.73
  39.8 0.5 fusion.73
  41.2 0.5 fusion.73
  42.6 0.5 fusion.73
  44.0 0.5 fusion.73
  45.4 0.5 fusion.73
  46.8 0.5 fusion.73
  48.2 0.5 fusion.73
  49.6 0.5 fusion.73
  51.0 0.5 fusion.73
  51.6 0.7 broadcast_in_dim.58
  52.3 3.8 %all-to-all-start.1 = ((f32[32,6,256]{2,1,0:T(8,128)}), f32[32,6,256]{2,1,0:T(8,128)S(1)}, u32[]{:S(2)}, u32[]{:S(2)}) async-start(f32[32,6,256]{2,1,0:T(8,128)} %broadcast_in_dim.58), calls=%async_computation.1 | async-start | bytes 524288 | tf_op jit(solution)/shard_map/all_to_all | solution.py:16
  56.1 13.2 %all-to-all-done.1 = f32[32,6,256]{2,1,0:T(8,128)S(1)} async-done(((f32[32,6,256]{2,1,0:T(8,128)}), f32[32,6,256]{2,1,0:T(8,128)S(1)}, u32[]{:S(2)}, u32[]{:S(2)}) %all-to-all-start.1) | async-done | bytes 196640 | tf_op jit(solution)/shard_map/all_to_all | solution.py:16
  69.4 22.4 %while.67 = (s32[]{:T(128)}, f32[3,256]{1,0:T(4,128)S(1)}, f32[3,256]{1,0:T(4,128)S(1)}, f32[16,3,512]{2,1,0:T(4,128)S(1)}, f32[16,3,512]{2,1,0:T(4,128)S(1)}, /*index=5*/s32[]{:T(128)}, s32[]{:T(128)}) while((s32[]{:T(128)}, f32[3,256]{1,0:T(4,128)S(1)}, f32[3,256]{1,0:T(4,128)S(1)}, f32[16,3,512]{2,1,0:T(4,128)S(1)}, ...), condition=%wide.region_9.10_spmd.clone, body=%wide.region_5.9_spmd.clone.sunk | while | flops 6161155 | bytes 4261979 | solution.py:88
  70.3 0.5 fusion.75
  71.7 0.5 fusion.75
  73.1 0.5 fusion.75
  74.5 0.5 fusion.75
  75.9 0.5 fusion.75
  77.3 0.5 fusion.75
  78.6 0.5 fusion.75
  80.0 0.5 fusion.75
  81.4 0.5 fusion.75
  82.8 0.5 fusion.75
  84.2 0.5 fusion.75
  85.6 0.5 fusion.75
  87.0 0.5 fusion.75
  88.4 0.5 fusion.75
  89.8 0.5 fusion.75
  91.2 0.5 fusion.75
  91.8 0.7 broadcast_in_dim.59
  92.5 4.1 %all-to-all-start.2 = ((f32[32,6,256]{2,1,0:T(8,128)}), f32[32,6,256]{2,1,0:T(8,128)S(1)}, u32[]{:S(2)}, u32[]{:S(2)}) async-start(f32[32,6,256]{2,1,0:T(8,128)} %broadcast_in_dim.59), calls=%async_computation.2 | async-start | bytes 524288 | tf_op jit(solution)/shard_map/all_to_all | solution.py:16
  96.6 12.9 %all-to-all-done.2 = f32[32,6,256]{2,1,0:T(8,128)S(1)} async-done(((f32[32,6,256]{2,1,0:T(8,128)}), f32[32,6,256]{2,1,0:T(8,128)S(1)}, u32[]{:S(2)}, u32[]{:S(2)}) %all-to-all-start.2) | async-done | bytes 196640 | tf_op jit(solution)/shard_map/all_to_all | solution.py:16
  109.6 22.4 %while.68 = (s32[]{:T(128)}, f32[3,256]{1,0:T(4,128)S(1)}, f32[3,256]{1,0:T(4,128)S(1)}, f32[16,3,512]{2,1,0:T(4,128)S(1)}, f32[16,3,512]{2,1,0:T(4,128)S(1)}, /*index=5*/s32[]{:T(128)}, s32[]{:T(128)}) while((s32[]{:T(128)}, f32[3,256]{1,0:T(4,128)S(1)}, f32[3,256]{1,0:T(4,128)S(1)}, f32[16,3,512]{2,1,0:T(4,128)S(1)}, ...), condition=%wide.region_14.15_spmd.clone, body=%wide.region_10.14_spmd.clone.sunk | while | flops 6161155 | bytes 4261979 | solution.py:88
  132.0 0.7 broadcast_in_dim.60
  132.7 4.6 %all-to-all-start.3 = ((f32[32,6,256]{2,1,0:T(8,128)}), f32[32,6,256]{2,1,0:T(8,128)S(1)}, u32[]{:S(2)}, u32[]{:S(2)}) async-start(f32[32,6,256]{2,1,0:T(8,128)} %broadcast_in_dim.60), calls=%async_computation.3 | async-start | bytes 524288 | tf_op jit(solution)/shard_map/all_to_all | solution.py:16
  137.4 12.8 %all-to-all-done.3 = f32[32,6,256]{2,1,0:T(8,128)S(1)} async-done(((f32[32,6,256]{2,1,0:T(8,128)}), f32[32,6,256]{2,1,0:T(8,128)S(1)}, u32[]{:S(2)}, u32[]{:S(2)}) %all-to-all-start.3) | async-done | bytes 196640 | tf_op jit(solution)/shard_map/all_to_all | solution.py:16
  150.2 22.4 %while.69 = (s32[]{:T(128)}, f32[3,256]{1,0:T(4,128)S(1)}, f32[3,256]{1,0:T(4,128)S(1)}, f32[16,3,512]{2,1,0:T(4,128)S(1)}, f32[16,3,512]{2,1,0:T(4,128)S(1)}, /*index=5*/s32[]{:T(128)}, s32[]{:T(128)}) while((s32[]{:T(128)}, f32[3,256]{1,0:T(4,128)S(1)}, f32[3,256]{1,0:T(4,128)S(1)}, f32[16,3,512]{2,1,0:T(4,128)S(1)}, ...), condition=%wide.region_19.20_spmd.clone, body=%wide.region_15.19_spmd.clone.sunk | while | flops 6161155 | bytes 4261979 | solution.py:88
  151.1 0.5 fusion.79
  152.5 0.5 fusion.79
  153.9 0.5 fusion.79
  172.6 0.7 broadcast_in_dim.67
  173.3 4.3 %all-to-all-start.4 = ((f32[32,6,256]{2,1,0:T(8,128)}), f32[32,6,256]{2,1,0:T(8,128)S(1)}, u32[]{:S(2)}, u32[]{:S(2)}) async-start(f32[32,6,256]{2,1,0:T(8,128)} %broadcast_in_dim.67), calls=%async_computation.4 | async-start | bytes 524288 | tf_op jit(solution)/shard_map/all_to_all | solution.py:16
  177.7 12.8 %all-to-all-done.4 = f32[32,6,256]{2,1,0:T(8,128)S(1)} async-done(((f32[32,6,256]{2,1,0:T(8,128)}), f32[32,6,256]{2,1,0:T(8,128)S(1)}, u32[]{:S(2)}, u32[]{:S(2)}) %all-to-all-start.4) | async-done | bytes 196640 | tf_op jit(solution)/shard_map/all_to_all | solution.py:16
  190.5 22.3 %while.70 = (s32[]{:T(128)}, f32[3,256]{1,0:T(4,128)S(1)}, f32[3,256]{1,0:T(4,128)S(1)}, f32[16,3,512]{2,1,0:T(4,128)S(1)}, f32[16,3,512]{2,1,0:T(4,128)S(1)}, /*index=5*/s32[]{:T(128)}, s32[]{:T(128)}) while((s32[]{:T(128)}, f32[3,256]{1,0:T(4,128)S(1)}, f32[3,256]{1,0:T(4,128)S(1)}, f32[16,3,512]{2,1,0:T(4,128)S(1)}, ...), condition=%wide.region_24.25_spmd.clone, body=%wide.region_20.24_spmd.clone.sunk | while | flops 6161155 | bytes 4261979 | solution.py:88
  212.8 0.7 broadcast_in_dim.68
  213.5 4.3 %all-to-all-start.5 = ((f32[32,6,256]{2,1,0:T(8,128)}), f32[32,6,256]{2,1,0:T(8,128)S(1)}, u32[]{:S(2)}, u32[]{:S(2)}) async-start(f32[32,6,256]{2,1,0:T(8,128)} %broadcast_in_dim.68), calls=%async_computation.5 | async-start | bytes 524288 | tf_op jit(solution)/shard_map/all_to_all | solution.py:16
  217.9 12.8 %all-to-all-done.5 = f32[32,6,256]{2,1,0:T(8,128)S(1)} async-done(((f32[32,6,256]{2,1,0:T(8,128)}), f32[32,6,256]{2,1,0:T(8,128)S(1)}, u32[]{:S(2)}, u32[]{:S(2)}) %all-to-all-start.5) | async-done | bytes 196640 | tf_op jit(solution)/shard_map/all_to_all | solution.py:16
  230.7 22.4 %while.71 = (s32[]{:T(128)}, f32[3,256]{1,0:T(4,128)S(1)}, f32[3,256]{1,0:T(4,128)S(1)}, f32[16,3,512]{2,1,0:T(4,128)S(1)}, f32[16,3,512]{2,1,0:T(4,128)S(1)}, /*index=5*/s32[]{:T(128)}, s32[]{:T(128)}) while((s32[]{:T(128)}, f32[3,256]{1,0:T(4,128)S(1)}, f32[3,256]{1,0:T(4,128)S(1)}, f32[16,3,512]{2,1,0:T(4,128)S(1)}, ...), condition=%wide.region_29.30_spmd.clone, body=%wide.region_25.29_spmd.clone.sunk | while | flops 6161155 | bytes 4261979 | solution.py:88
  253.1 0.6 fusion.53
  253.9 13.7 %all_to_all.36 = f32[32,1,256]{2,1,0:T(1,128)S(1)} all-to-all(f32[32,1,256]{2,1,0:T(1,128)S(1)} %broadcast_in_dim.69), channel_id=1, replica_groups=mesh['rep'=8,'blk'=32] {'blk'}, dimensions={0} | all-to-all | bytes 65536 | tf_op jit(solution)/shard_map/all_to_all | solution.py:16
  267.7 0.8 convolution_multiply_fusion
  (484 shorter events, 113.1 us)
Async XLA Ops:
  2.8 26.3 %copy-start = (f32[3,256]{1,0:T(4,128)S(1)}, f32[3,256]{1,0:T(4,128)}, u32[]{:S(2)}) copy-start(f32[3,256]{1,0:T(4,128)} %param.18) | copy-start | bytes 9220
  2.8 26.3 %all-to-all-start = ((f32[32,6,256]{2,1,0:T(8,128)}), f32[32,6,256]{2,1,0:T(8,128)S(1)}, u32[]{:S(2)}, u32[]{:S(2)}) async-start(f32[32,6,256]{2,1,0:T(8,128)} %broadcast_in_dim.57), calls=%async_computation | async-start | bytes 524288 | tf_op jit(solution)/shard_map/all_to_all | solution.py:16
  29.1 22.4 %copy-start.4 = (f32[6,3,256]{2,1,0:T(4,128)S(1)}, f32[6,3,256]{2,1,0:T(4,128)}, u32[]{:S(2)}) copy-start(f32[6,3,256]{2,1,0:T(4,128)} %param.20) | copy-start | bytes 55300
  52.3 17.0 %all-to-all-start.1 = ((f32[32,6,256]{2,1,0:T(8,128)}), f32[32,6,256]{2,1,0:T(8,128)S(1)}, u32[]{:S(2)}, u32[]{:S(2)}) async-start(f32[32,6,256]{2,1,0:T(8,128)} %broadcast_in_dim.58), calls=%async_computation.1 | async-start | bytes 524288 | tf_op jit(solution)/shard_map/all_to_all | solution.py:16
  92.5 17.1 %all-to-all-start.2 = ((f32[32,6,256]{2,1,0:T(8,128)}), f32[32,6,256]{2,1,0:T(8,128)S(1)}, u32[]{:S(2)}, u32[]{:S(2)}) async-start(f32[32,6,256]{2,1,0:T(8,128)} %broadcast_in_dim.59), calls=%async_computation.2 | async-start | bytes 524288 | tf_op jit(solution)/shard_map/all_to_all | solution.py:16
  132.7 17.5 %all-to-all-start.3 = ((f32[32,6,256]{2,1,0:T(8,128)}), f32[32,6,256]{2,1,0:T(8,128)S(1)}, u32[]{:S(2)}, u32[]{:S(2)}) async-start(f32[32,6,256]{2,1,0:T(8,128)} %broadcast_in_dim.60), calls=%async_computation.3 | async-start | bytes 524288 | tf_op jit(solution)/shard_map/all_to_all | solution.py:16
  173.3 17.1 %all-to-all-start.4 = ((f32[32,6,256]{2,1,0:T(8,128)}), f32[32,6,256]{2,1,0:T(8,128)S(1)}, u32[]{:S(2)}, u32[]{:S(2)}) async-start(f32[32,6,256]{2,1,0:T(8,128)} %broadcast_in_dim.67), calls=%async_computation.4 | async-start | bytes 524288 | tf_op jit(solution)/shard_map/all_to_all | solution.py:16
  213.5 17.1 %all-to-all-start.5 = ((f32[32,6,256]{2,1,0:T(8,128)}), f32[32,6,256]{2,1,0:T(8,128)S(1)}, u32[]{:S(2)}, u32[]{:S(2)}) async-start(f32[32,6,256]{2,1,0:T(8,128)} %broadcast_in_dim.68), calls=%async_computation.5 | async-start | bytes 524288 | tf_op jit(solution)/shard_map/all_to_all | solution.py:16
  230.7 23.0 %copy-start.1 = (f32[128,3,256]{2,0,1:T(8,128)S(1)}, f32[128,3,256]{2,0,1:T(8,128)}, u32[]{:S(2)}) copy-start(f32[128,3,256]{2,0,1:T(8,128)} %param.22) | copy-start | bytes 1179652
  230.7 23.0 %copy-start.2 = (f32[128,3,256]{2,0,1:T(8,128)S(1)}, f32[128,3,256]{2,0,1:T(8,128)}, u32[]{:S(2)}) copy-start(f32[128,3,256]{2,0,1:T(8,128)} %param.21) | copy-start | bytes 1179652
  253.1 15.5 %copy-start.3 = (f32[3,256]{1,0:T(4,128)}, f32[3,256]{1,0:T(4,128)S(1)}, u32[]{:S(2)}) copy-start(f32[3,256]{1,0:T(4,128)S(1)} %get-tuple-element.163) | copy-start | bytes 9220
  253.1 14.6 %copy-start.5 = (s32[128]{0:T(128)S(1)}, s32[128]{0:T(128)}, u32[]{:S(2)}) copy-start(s32[128]{0:T(128)} %param.23) | copy-start | bytes 1540
where the time goes:
time: 269 us
  other arithmetic  130 us (48%)
  waiting for transfers between devices  77.8 us (29%)
  starting transfers between devices  34 us (13%)
  blocking collectives  13.7 us (5%)
  local copies, waits for them, and re-layouts  6.37 us (2%)
  loops' own time  4.64 us (2%)
    all_to_all x6, waiting for transfers between devices, sent_to_all(): return lax.all_to_all(copies, axis, split_axis=0, concat_axis=0, tiled=True)  77.8 us
    reduce_sum x96, other arithmetic, pair_velocity(): jnp.sum(coef_iso[None] * loads[:, :, None] + (coef_dir * projection)[None...  46.8 us
    reduce_sum x96, other arithmetic, pair_coefs(): dist_sq = jnp.sum(separation * separation, axis=0)  45.3 us
    select_n x96, other arithmetic, pair_coefs(): jnp.where(far_mask, 0.75 * inv_dist * (1.0 + 2.0 / 3.0 * inv_sq), 1.0 - 9...  35.3 us
    all_to_all x6, starting transfers between devices, sent_to_all(): return lax.all_to_all(copies, axis, split_axis=0, concat_axis=0, tiled=True)  34 us
    all_to_all x1, blocking collectives, sent_to_all(): return lax.all_to_all(copies, axis, split_axis=0, concat_axis=0, tiled=True)  13.7 us
  transfers between devices with their start and end apart: 6, of which 6 were waited for; matrix products, arithmetic and copies ran while one was open for 0% of the time, Pallas kernels for 0%

commit v1 on v0

v1 whole, which is shorter than its diff:
```python
import jax
import jax.numpy as jnp
from jax import lax
from jax.experimental import pallas as pl
from jax.experimental.pallas import tpu as pltpu
from jax.sharding import PartitionSpec as P

STEPS = 6
BLK = 256
KROWS = 64
PAIR = 2
CHUNK = 32
BF = jnp.bfloat16
F32 = jnp.float32

time_step = 0.05
CENTRE = 32.0
SIGMA = 0.75**0.5
ROOT3 = 3.0**0.5
ALPHA = 9.0 / (32.0 * SIGMA)
BETA = 1.125 * SIGMA


def halves(a):
    hi = a.astype(BF).astype(F32)
    return hi, a - hi


def thirds(a):
    hi, rest = halves(a)
    mid, low = halves(rest)
    return hi, mid, low


def split_place(x):
    scaled = (x - CENTRE) * SIGMA
    hi = (jnp.round(scaled * 8.0) * 0.125).astype(BF).astype(F32)
    mid = (scaled - hi).astype(BF).astype(F32)
    return hi, mid


def feature_rows(hi, mid):
    hh = hi[0] * hi[0] + hi[1] * hi[1] + hi[2] * hi[2]
    hm = 2.0 * (hi[0] * mid[0] + hi[1] * mid[1] + hi[2] * mid[2])
    mm = mid[0] * mid[0] + mid[1] * mid[1] + mid[2] * mid[2]
    return thirds(hh), thirds(hm), halves(mm)


def source_table(x, f):
    hi, mid = zip(*(split_place(a) for a in x))
    fh = [a.astype(BF).astype(F32) for a in f]
    fm = [(a - b).astype(BF).astype(F32) for a, b in zip(f, fh)]
    hh, hm, mm = feature_rows(hi, mid)
    along = thirds(sum((h + m) * (a + b) for h, m, a, b in zip(hi, mid, fh, fm)))
    one, zero = jnp.ones_like(hi[0]), jnp.zeros_like(hi[0])
    minus_hi = [-2.0 * a for a in hi]
    minus_mid = [-2.0 * a for a in mid]
    rows = [*minus_hi, *hh, one, one, one] + [zero] * 7
    rows += [*minus_hi, *minus_mid, *hm, one, one, one] + [zero] * 4
    rows += [*minus_mid, *mm, one, one, zero]
    rows += [*fh, *fm, *fh, *fm, *along] + [zero] * 9
    weights = [*fh, *fm, *hi, *mid, one, zero, zero, zero]
    return rows, weights


def target_table(hi, mid):
    h, m = [hi[c : c + 1] for c in range(3)], [mid[c : c + 1] for c in range(3)]
    hh, hm, mm = feature_rows(h, m)
    one, zero = jnp.ones_like(h[0]), jnp.zeros_like(h[0])
    dist = [*h, one, one, one, *hh] + [zero] * 7
    dist += [*m, *h, one, one, one, *hm] + [zero] * 4
    dist += [*m, one, one, *mm, zero] + [zero] * 24
    proj = [zero] * 40 + [*h, *h, *m, *m, -one, -one, -one] + [zero] * 9
    return jnp.concatenate(
        [jnp.concatenate(dist, axis=0), jnp.concatenate(proj, axis=0)], axis=1
    ).astype(BF)


def pair_kernel(blocks, xs_ref, fs_ref, own_ref, kick_ref, place_ref, vel_ref, rows_ref, weights_ref,
                even_ref, odd_ref, even_coef_ref, odd_coef_ref):
    def spread(ref, groups_of_8, group, k, row):
        at = ((group // 8) * groups_of_8 + k // 8) * 64 + k % 8
        for half in range(2):
            ref[half, pl.ds(at, 8, stride=8), :] = row[:, half * 128 : half * 128 + 128]

    for group in range(0, blocks, 8):
        part = pl.ds(group, 8)
        x = [xs_ref[part, c * BLK : (c + 1) * BLK] for c in range(3)]
        f = [fs_ref[part, c * BLK : (c + 1) * BLK] for c in range(3)]
        rows, weights = source_table(x, f)
        for k, row in enumerate(rows):
            spread(rows_ref, KROWS // 8, group, k, row)
        for k, row in enumerate(weights):
            spread(weights_ref, 2, group, k, row)

    own = own_ref[...]
    hi, mid = split_place(own)
    table = target_table(hi, mid)

    def block_rows(ref, groups_of_8, b, half):
        at = ((b // 8) * groups_of_8 * 8 + b % 8) * 8
        return jnp.concatenate(
            [ref[half, pl.ds(pl.multiple_of(at + g * 64, 8), 8), :] for g in range(groups_of_8)], axis=0
        ).astype(BF)

    def geometry(b0, both_ref):
        lhs = jnp.concatenate(
            [block_rows(rows_ref, KROWS // 8, b0 + n, h).T for n in range(PAIR) for h in range(2)], axis=0
        )
        both_ref[...] = jnp.dot(lhs, table, preferred_element_type=F32)

    def coefficients(both_ref, coef_ref):
        for at in range(0, PAIR * BLK, CHUNK):
            rows = slice(at, at + CHUNK)
            dist_sq = jnp.maximum(both_ref[rows, :BLK], 1e-8)
            along = both_ref[rows, BLK:]
            inv = lax.rsqrt(dist_sq)
            inv_far = jnp.minimum(inv, 1.0 / ROOT3)
            inv_sq = inv_far * inv_far
            iso = inv_far * (2.0 + inv_sq) + jnp.maximum(ROOT3 - dist_sq * inv, 0.0)
            pull = inv * (inv_sq * (2.0 / 3.0 - inv_sq)) * along
            iso_hi = iso.astype(BF)
            pull_hi = pull.astype(BF)
            coef_ref[0, rows, :] = iso_hi
            coef_ref[1, rows, :] = (iso - iso_hi.astype(F32)).astype(BF)
            coef_ref[2, rows, :] = pull_hi
            coef_ref[3, rows, :] = (pull - pull_hi.astype(F32)).astype(BF)

    def totals(b0, coef_ref, sums):
        w = jnp.concatenate(
            [block_rows(weights_ref, 2, b0 + n, h) for n in range(PAIR) for h in range(2)], axis=1
        )
        dot = lambda a: jnp.dot(w, a, preferred_element_type=F32)
        return (
            sums[0] + (dot(coef_ref[0]) + dot(coef_ref[1])),
            sums[1] + (dot(coef_ref[2]) + dot(coef_ref[3])),
        )

    def trip(i, sums):
        b0 = i * (2 * PAIR)
        geometry(b0 + PAIR, odd_ref)
        coefficients(even_ref, even_coef_ref)
        sums = totals(jnp.maximum(b0 - PAIR, 0), odd_coef_ref, sums)
        geometry(jnp.minimum(b0 + 2 * PAIR, blocks - PAIR), even_ref)
        coefficients(odd_ref, odd_coef_ref)
        sums = totals(b0, even_coef_ref, sums)
        return sums

    nothing = jnp.zeros((16, BLK), F32)
    odd_coef_ref[...] = jnp.zeros_like(odd_coef_ref)
    geometry(0, even_ref)
    sums = lax.fori_loop(0, blocks // (2 * PAIR), trip, (nothing, nothing))
    iso_sum, pull_sum = totals(blocks - PAIR, odd_coef_ref, sums)
    vel = ALPHA * (iso_sum[0:3] + iso_sum[3:6]) + BETA * (
        (hi + mid) * pull_sum[12:13] - (pull_sum[6:9] + pull_sum[9:12])
    )
    vel_ref[...] = vel
    place_ref[...] = own + time_step * vel + kick_ref[...]


def pair_step(xs, fs, own, kick):
    blocks = xs.shape[0]
    vmem = pl.BlockSpec(memory_space=pltpu.VMEM)
    out = jax.ShapeDtypeStruct(own.shape, F32)
    return pl.pallas_call(
        lambda *refs: pair_kernel(blocks, *refs),
        out_shape=(out, out),
        in_specs=[vmem] * 4,
        out_specs=(vmem, vmem),
        scratch_shapes=[
            pltpu.VMEM((2, blocks * KROWS, 128), F32),
            pltpu.VMEM((2, blocks * 16, 128), F32),
            pltpu.VMEM((PAIR * BLK, 2 * BLK), F32),
            pltpu.VMEM((PAIR * BLK, 2 * BLK), F32),
            pltpu.VMEM((4, PAIR * BLK, BLK), BF),
            pltpu.VMEM((4, PAIR * BLK, BLK), BF),
        ],
        cost_estimate=pl.CostEstimate(flops=10**8, bytes_accessed=10**6, transcendentals=0),
        compiler_params=pltpu.CompilerParams(vmem_limit_bytes=40 * 2**20),
        name="pair_step",
    )(xs, fs, own, kick)


def sent_to_all(x, axis):
    copies = jnp.broadcast_to(x, (lax.axis_size(axis), *x.shape))
    return lax.all_to_all(copies, axis, split_axis=0, concat_axis=0, tiled=True)


def local(positions, forces, random_kicks, history_velocity, history_offset, lag_index):
    places = positions
    width = 3 * BLK
    first = jnp.concatenate([positions.reshape(-1), forces.reshape(-1)])
    everything = sent_to_all(first, "blk")
    blocks = everything.shape[0]
    for step in range(STEPS):
        if step == 0:
            xs = everything[:, :width]
        else:
            xs = sent_to_all(places.reshape(-1), "blk")
        fs = everything[:, (step + 1) * width : (step + 2) * width]
        places, velocity = pair_step(xs, fs, places, random_kicks[step])
    velocity_dot = jnp.sum(velocity[None] * history_velocity, axis=(1, 2))
    moved = places[None] - positions[None] - history_offset
    square_disp = jnp.sum(moved * moved, axis=(1, 2))
    frames = history_velocity.shape[0]
    sphere_total = jnp.float32(positions.shape[1] * blocks)
    sums = jnp.sum(sent_to_all(jnp.concatenate([velocity_dot, square_disp]), "blk"), axis=0)
    frame_table = jnp.stack([sums[:frames], sums[frames:]], axis=1)
    onehot = (lag_index[:, None] == jnp.arange(frames, dtype=jnp.int32)[None, :]).astype(F32)
    picked = jnp.dot(onehot, frame_table, precision=lax.Precision.HIGHEST, preferred_element_type=F32)
    statistics = picked.T / sphere_total
    return (places, velocity, statistics)


def solution(mesh):
    return jax.shard_map(
        local,
        mesh=mesh,
        in_specs=(
            P(None, ("rep", "blk")),
            P(None, None, ("rep", "blk")),
            P(None, None, ("rep", "blk")),
            P(None, None, ("rep", "blk")),
            P(None, None, ("rep", "blk")),
            P(("rep", "blk")),
        ),
        out_specs=(P(None, ("rep", "blk")), P(None, ("rep", "blk")), P(None, ("rep", "blk"))),
        check_vma=False,
    )
```

time: 269 us -> 187 us (0.70)
  other arithmetic: 130 us -> 0.92 us
  blocking collectives: 13.7 us -> 82.4 us
  Pallas kernels: 0 us -> 64.8 us
  waiting for transfers between devices: 77.8 us -> 20.8 us
  starting transfers between devices: 34 us -> 12.9 us
  loops' own time: 4.64 us -> 0 us
  local copies, waits for them, and re-layouts: 6.37 us -> 3.13 us
    reduce_sum x193 -> x1, other arithmetic: 92.2 us -> 0.05 us  [local(): jnp.sum(sent_to_all(jnp.concatenate([velocity_dot, square_disp]), 'blk'),...]
    all_to_all x1 -> x6, blocking collectives: 13.7 us -> 82.4 us  [sent_to_all(): return lax.all_to_all(copies, axis, split_axis=0, concat_axis=0, tiled=True)]
    pallas_call x0 -> x6, Pallas kernels: none -> 64.8 us  [pair_step(): pl.pallas_call(lambda *refs: pair_kernel(blocks, *refs), out_shape=(out,...]
    all_to_all x6 -> x1, waiting for transfers between devices: 77.8 us -> 20.8 us  [sent_to_all(): return lax.all_to_all(copies, axis, split_axis=0, concat_axis=0, tiled=True)]
    select_n x96 -> x0, other arithmetic: 35.3 us -> none  [pair_coefs(): jnp.where(far_mask, 0.75 * inv_dist * (1.0 + 2.0 / 3.0 * inv_sq), 1.0 - 9...]
    all_to_all x6 -> x1, starting transfers between devices: 34 us -> 12.9 us  [sent_to_all(): return lax.all_to_all(copies, axis, split_axis=0, concat_axis=0, tiled=True)]
    another operation x6 -> x0, loops' own time: 4.64 us -> none  [blockwise(): lax.scan(accumulate, jnp.zeros(targets.shape, jnp.float32), (source_block...]
    broadcast_in_dim x7 -> x12, local copies, waits for them, and re-layouts: 4.28 us -> 1.54 us  [sent_to_all(): copies = jnp.broadcast_to(x, (lax.axis_size(axis), *x.shape))]
  transfers between devices with their start and end apart: 6 -> 1, of which waited for: 6 -> 1; matrix products, arithmetic and copies ran while one was open for 0% -> 0% of each run, Pallas kernels for 0% -> 0%
where the time goes in v1:
time: 187 us
  blocking collectives  82.4 us (44%)
  Pallas kernels  64.8 us (35%)
  waiting for transfers between devices  20.8 us (11%)
  starting transfers between devices  12.9 us (7%)
  local copies, waits for them, and re-layouts  3.13 us (2%)
    all_to_all x6, blocking collectives, sent_to_all(): return lax.all_to_all(copies, axis, split_axis=0, concat_axis=0, tiled=True)  82.4 us
    pallas_call x6, Pallas kernels, pair_step(): pl.pallas_call(lambda *refs: pair_kernel(blocks, *refs), out_shape=(out,...  64.8 us
    all_to_all x1, waiting for transfers between devices, sent_to_all(): return lax.all_to_all(copies, axis, split_axis=0, concat_axis=0, tiled=True)  20.8 us
    all_to_all x1, starting transfers between devices, sent_to_all(): return lax.all_to_all(copies, axis, split_axis=0, concat_axis=0, tiled=True)  12.9 us
  transfers between devices with their start and end apart: 1, of which 1 were waited for; matrix products, arithmetic and copies ran while one was open for 0% of the time, Pallas kernels for 0%

profile of v1, /device:TPU:1, one launch (start us, length us, event | category | flops | bytes accessed | tf_op | source)
XLA Modules:
  0.0 186.5 jit_solution(4520895505069812814)
XLA Ops:
  0.6 0.0 copy-start
  0.6 0.8 reshape.65
  1.4 0.0 copy-done
  1.4 1.2 broadcast_in_dim.36
  2.6 0.0 copy-start.3
  2.6 12.9 %all-to-all-start = ((f32[32,1,5376]{2,1,0:T(1,128)}), f32[32,1,5376]{2,1,0:T(1,128)S(1)}, u32[]{:S(2)}, u32[]{:S(2)}) async-start(f32[32,1,5376]{2,1,0:T(1,128)} %broadcast_in_dim.36), calls=%async_computation | async-start | bytes 1376256 | tf_op jit(solution)/shard_map/all_to_all | solution.py:186
  15.5 0.0 copy-done.3
  15.5 20.8 %all-to-all-done = f32[32,1,5376]{2,1,0:T(1,128)S(1)} async-done(((f32[32,1,5376]{2,1,0:T(1,128)}), f32[32,1,5376]{2,1,0:T(1,128)S(1)}, u32[]{:S(2)}, u32[]{:S(2)}) %all-to-all-start) | async-done | bytes 688160 | tf_op jit(solution)/shard_map/all_to_all | solution.py:186
  36.4 0.1 fusion.5
  36.5 10.8 %pair_step.6 = (f32[3,256]{1,0:T(4,128)S(1)}, f32[3,256]{1,0:T(4,128)}) custom-call(f32[32,768]{1,0:T(8,128)S(1)} %get-tuple-element.23.refs_0_, f32[32,768]{1,0:T(8,128)S(1)} %get-tuple-element.22.refs_1_, f32[3,256]{1,0:T(4,128)S(1)} %copy-done, f32[3,256]{1,0:T(4,128)S(1)} %get-tuple-element.28.refs_3_), custom_call_target="tpu_custom_call" | custom-call | flops 100000000 | bytes 1000000 | tf_op jit(solution)/shard_map/pair_step/pallas_call | solution.py:165
  47.3 0.1 broadcast_in_dim.38
  47.3 15.5 %all_to_all.55 = f32[32,1,768]{2,1,0:T(1,128)S(1)} all-to-all(f32[32,1,768]{2,1,0:T(1,128)S(1)} %broadcast_in_dim.38), channel_id=1, replica_groups=mesh['rep'=8,'blk'=32] {'blk'}, dimensions={0} | all-to-all | bytes 196608 | tf_op jit(solution)/shard_map/all_to_all | solution.py:186
  62.8 10.8 %pair_step.7 = (f32[3,256]{1,0:T(4,128)S(1)}, f32[3,256]{1,0:T(4,128)}) custom-call(f32[32,768]{1,0:T(8,128)S(1)} %bitcast.35, f32[32,768]{1,0:T(8,128)S(1)} %get-tuple-element.21.refs_1_, f32[3,256]{1,0:T(4,128)S(1)} %get-tuple-element.10.refs_2_, f32[3,256]{1,0:T(4,128)S(1)} %get-tuple-element.27.refs_3_), custom_call_target="tpu_custom_call" | custom-call | flops 100000000 | bytes 1000000 | tf_op jit(solution)/shard_map/pair_step/pallas_call | solution.py:165
  73.6 0.1 broadcast_in_dim.40
  73.7 13.5 %all_to_all.56 = f32[32,1,768]{2,1,0:T(1,128)S(1)} all-to-all(f32[32,1,768]{2,1,0:T(1,128)S(1)} %broadcast_in_dim.40), channel_id=1, replica_groups=mesh['rep'=8,'blk'=32] {'blk'}, dimensions={0} | all-to-all | bytes 196608 | tf_op jit(solution)/shard_map/all_to_all | solution.py:186
  87.2 10.8 %pair_step.8 = (f32[3,256]{1,0:T(4,128)S(1)}, f32[3,256]{1,0:T(4,128)}) custom-call(f32[32,768]{1,0:T(8,128)S(1)} %bitcast.36, f32[32,768]{1,0:T(8,128)S(1)} %get-tuple-element.20.refs_1_, f32[3,256]{1,0:T(4,128)S(1)} %get-tuple-element.11.refs_2_, f32[3,256]{1,0:T(4,128)S(1)} %get-tuple-element.26.refs_3_), custom_call_target="tpu_custom_call" | custom-call | flops 100000000 | bytes 1000000 | tf_op jit(solution)/shard_map/pair_step/pallas_call | solution.py:165
  98.0 0.1 broadcast_in_dim.42
  98.1 13.5 %all_to_all.57 = f32[32,1,768]{2,1,0:T(1,128)S(1)} all-to-all(f32[32,1,768]{2,1,0:T(1,128)S(1)} %broadcast_in_dim.42), channel_id=1, replica_groups=mesh['rep'=8,'blk'=32] {'blk'}, dimensions={0} | all-to-all | bytes 196608 | tf_op jit(solution)/shard_map/all_to_all | solution.py:186
  111.6 10.8 %pair_step.9 = (f32[3,256]{1,0:T(4,128)S(1)}, f32[3,256]{1,0:T(4,128)}) custom-call(f32[32,768]{1,0:T(8,128)S(1)} %bitcast.37, f32[32,768]{1,0:T(8,128)S(1)} %get-tuple-element.19.refs_1_, f32[3,256]{1,0:T(4,128)S(1)} %get-tuple-element.12.refs_2_, f32[3,256]{1,0:T(4,128)S(1)} %get-tuple-element.25.refs_3_), custom_call_target="tpu_custom_call" | custom-call | flops 100000000 | bytes 1000000 | tf_op jit(solution)/shard_map/pair_step/pallas_call | solution.py:165
  122.4 0.1 broadcast_in_dim.44
  122.5 13.5 %all_to_all.58 = f32[32,1,768]{2,1,0:T(1,128)S(1)} all-to-all(f32[32,1,768]{2,1,0:T(1,128)S(1)} %broadcast_in_dim.44), channel_id=1, replica_groups=mesh['rep'=8,'blk'=32] {'blk'}, dimensions={0} | all-to-all | bytes 196608 | tf_op jit(solution)/shard_map/all_to_all | solution.py:186
  136.0 10.8 %pair_step.10 = (f32[3,256]{1,0:T(4,128)S(1)}, f32[3,256]{1,0:T(4,128)}) custom-call(f32[32,768]{1,0:T(8,128)S(1)} %bitcast.38, f32[32,768]{1,0:T(8,128)S(1)} %get-tuple-element.18.refs_1_, f32[3,256]{1,0:T(4,128)S(1)} %get-tuple-element.13.refs_2_, f32[3,256]{1,0:T(4,128)S(1)} %get-tuple-element.29.refs_3_), custom_call_target="tpu_custom_call" | custom-call | flops 100000000 | bytes 1000000 | tf_op jit(solution)/shard_map/pair_step/pallas_call | solution.py:165
  146.8 0.0 copy-start.2
  146.8 0.1 broadcast_in_dim.46
  146.8 0.0 copy-start.1
  146.9 13.6 %all_to_all.59 = f32[32,1,768]{2,1,0:T(1,128)S(1)} all-to-all(f32[32,1,768]{2,1,0:T(1,128)S(1)} %broadcast_in_dim.46), channel_id=1, replica_groups=mesh['rep'=8,'blk'=32] {'blk'}, dimensions={0} | all-to-all | bytes 196608 | tf_op jit(solution)/shard_map/all_to_all | solution.py:186
  160.5 10.8 %pair_step.11 = (f32[3,256]{1,0:T(4,128)}, f32[3,256]{1,0:T(4,128)}) custom-call(f32[32,768]{1,0:T(8,128)S(1)} %bitcast.34, f32[32,768]{1,0:T(8,128)S(1)} %get-tuple-element.17.refs_1_, f32[3,256]{1,0:T(4,128)S(1)} %get-tuple-element.14.refs_2_, f32[3,256]{1,0:T(4,128)S(1)} %get-tuple-element.24.refs_3_), custom_call_target="tpu_custom_call" | custom-call | flops 100000000 | bytes 1000000 | tf_op jit(solution)/shard_map/pair_step/pallas_call | solution.py:165
  171.3 0.0 copy-start.4
  171.3 0.7 sub.12
  172.0 0.0 copy-done.2
  172.0 0.0 copy-done.1
  172.0 0.0 copy-done.4
  172.0 0.1 multiply_reduce_fusion
  172.2 12.8 %all_to_all.60 = f32[32,1,256]{2,1,0:T(1,128)S(1)} all-to-all(f32[32,1,256]{2,1,0:T(1,128)S(1)} %broadcast_in_dim.47), channel_id=1, replica_groups=mesh['rep'=8,'blk'=32] {'blk'}, dimensions={0} | all-to-all | bytes 65536 | tf_op jit(solution)/shard_map/all_to_all | solution.py:186
  185.0 0.1 reduce_sum.29
  185.1 0.0 copy-start.5
  185.1 0.6 copy-done.5
  185.7 0.8 convolution_multiply_fusion
  (17 shorter events, 0.2 us)
Async XLA Ops:
  0.6 0.8 copy-start
  2.6 12.9 %copy-start.3 = (f32[6,3,256]{2,1,0:T(4,128)S(1)}, f32[6,3,256]{2,1,0:T(4,128)}, u32[]{:S(2)}) copy-start(f32[6,3,256]{2,1,0:T(4,128)} %param.8) | copy-start | bytes 55300
  2.6 33.7 %all-to-all-start = ((f32[32,1,5376]{2,1,0:T(1,128)}), f32[32,1,5376]{2,1,0:T(1,128)S(1)}, u32[]{:S(2)}, u32[]{:S(2)}) async-start(f32[32,1,5376]{2,1,0:T(1,128)} %broadcast_in_dim.36), calls=%async_computation | async-start | bytes 1376256 | tf_op jit(solution)/shard_map/all_to_all | solution.py:186
  146.8 25.2 %copy-start.2 = (f32[128,3,256]{2,0,1:T(8,128)S(1)}, f32[128,3,256]{2,0,1:T(8,128)}, u32[]{:S(2)}) copy-start(f32[128,3,256]{2,0,1:T(8,128)} %param.9) | copy-start | bytes 1179652
  146.8 25.2 %copy-start.1 = (f32[128,3,256]{2,0,1:T(8,128)S(1)}, f32[128,3,256]{2,0,1:T(8,128)}, u32[]{:S(2)}) copy-start(f32[128,3,256]{2,0,1:T(8,128)} %param.10) | copy-start | bytes 1179652
  171.3 0.7 copy-start.4
  185.1 0.7 copy-start.5

commit v2 on v1

--- a/solution.py
+++ b/solution.py
@@ -8,8 +8,9 @@
 STEPS = 6
 BLK = 256
 KROWS = 64
-PAIR = 2
-CHUNK = 32
+UNROLL = 16
+CHUNK = 128
+AHEAD = 3
 BF = jnp.bfloat16
 F32 = jnp.float32
 
@@ -76,8 +77,7 @@
     ).astype(BF)
 
 
-def pair_kernel(blocks, xs_ref, fs_ref, own_ref, kick_ref, place_ref, vel_ref, rows_ref, weights_ref,
-                even_ref, odd_ref, even_coef_ref, odd_coef_ref):
+def pair_kernel(blocks, xs_ref, fs_ref, own_ref, kick_ref, place_ref, vel_ref, rows_ref, weights_ref):
     def spread(ref, groups_of_8, group, k, row):
         at = ((group // 8) * groups_of_8 + k // 8) * 64 + k % 8
         for half in range(2):
@@ -103,54 +103,50 @@
             [ref[half, pl.ds(pl.multiple_of(at + g * 64, 8), 8), :] for g in range(groups_of_8)], axis=0
         ).astype(BF)
 
-    def geometry(b0, both_ref):
-        lhs = jnp.concatenate(
-            [block_rows(rows_ref, KROWS // 8, b0 + n, h).T for n in range(PAIR) for h in range(2)], axis=0
-        )
-        both_ref[...] = jnp.dot(lhs, table, preferred_element_type=F32)
-
-    def coefficients(both_ref, coef_ref):
-        for at in range(0, PAIR * BLK, CHUNK):
-            rows = slice(at, at + CHUNK)
-            dist_sq = jnp.maximum(both_ref[rows, :BLK], 1e-8)
-            along = both_ref[rows, BLK:]
-            inv = lax.rsqrt(dist_sq)
-            inv_far = jnp.minimum(inv, 1.0 / ROOT3)
-            inv_sq = inv_far * inv_far
-            iso = inv_far * (2.0 + inv_sq) + jnp.maximum(ROOT3 - dist_sq * inv, 0.0)
-            pull = inv * (inv_sq * (2.0 / 3.0 - inv_sq)) * along
-            iso_hi = iso.astype(BF)
-            pull_hi = pull.astype(BF)
-            coef_ref[0, rows, :] = iso_hi
-            coef_ref[1, rows, :] = (iso - iso_hi.astype(F32)).astype(BF)
-            coef_ref[2, rows, :] = pull_hi
-            coef_ref[3, rows, :] = (pull - pull_hi.astype(F32)).astype(BF)
-
-    def totals(b0, coef_ref, sums):
-        w = jnp.concatenate(
-            [block_rows(weights_ref, 2, b0 + n, h) for n in range(PAIR) for h in range(2)], axis=1
-        )
-        dot = lambda a: jnp.dot(w, a, preferred_element_type=F32)
-        return (
-            sums[0] + (dot(coef_ref[0]) + dot(coef_ref[1])),
-            sums[1] + (dot(coef_ref[2]) + dot(coef_ref[3])),
-        )
+    def source_columns(b):
+        return jnp.concatenate([block_rows(rows_ref, KROWS // 8, b, h).T for h in range(2)], axis=0)
+
+    def geometry(columns):
+        return jnp.dot(columns, table, preferred_element_type=F32)
+
+    def coefficients(both):
+        dist_sq = jnp.maximum(both[:, :BLK], 1e-8)
+        along = both[:, BLK:]
+        inv = lax.rsqrt(dist_sq)
+        inv_far = jnp.minimum(inv, 1.0 / ROOT3)
+        inv_sq = inv_far * inv_far
+        iso = inv_far * (2.0 + inv_sq) + jnp.maximum(ROOT3 - dist_sq * inv, 0.0)
+        pull = inv * (inv_sq * (2.0 / 3.0 - inv_sq)) * along
+        iso_hi = iso.astype(BF)
+        pull_hi = pull.astype(BF)
+        iso_lo = (iso - iso_hi.astype(F32)).astype(BF)
+        pull_lo = (pull - pull_hi.astype(F32)).astype(BF)
+        return iso_hi, iso_lo, pull_hi, pull_lo
+
+    def weight_rows(b):
+        return jnp.concatenate([block_rows(weights_ref, 2, b, h) for h in range(2)], axis=1)
 
     def trip(i, sums):
-        b0 = i * (2 * PAIR)
-        geometry(b0 + PAIR, odd_ref)
-        coefficients(even_ref, even_coef_ref)
-        sums = totals(jnp.maximum(b0 - PAIR, 0), odd_coef_ref, sums)
-        geometry(jnp.minimum(b0 + 2 * PAIR, blocks - PAIR), even_ref)
-        coefficients(odd_ref, odd_coef_ref)
-        sums = totals(b0, even_coef_ref, sums)
-        return sums
+        iso_sum, pull_sum = sums
+        b0 = i * UNROLL
+        pieces = BLK // CHUNK
+        columns = [source_columns(b0 + n) for n in range(UNROLL)]
+        at = lambda c: columns[c // pieces][(c % pieces) * CHUNK : (c % pieces + 1) * CHUNK]
+        ahead = [geometry(at(c)) for c in range(AHEAD)]
+        for c in range(UNROLL * pieces):
+            if c + AHEAD < UNROLL * pieces:
+                ahead.append(geometry(at(c + AHEAD)))
+            if c % pieces == 0:
+                w = weight_rows(b0 + c // pieces)
+            iso_hi, iso_lo, pull_hi, pull_lo = coefficients(ahead.pop(0))
+            piece = w[:, (c % pieces) * CHUNK : (c % pieces + 1) * CHUNK]
+            dot = lambda a: jnp.dot(piece, a, preferred_element_type=F32)
+            iso_sum = iso_sum + (dot(iso_hi) + dot(iso_lo))
+            pull_sum = pull_sum + (dot(pull_hi) + dot(pull_lo))
+        return iso_sum, pull_sum
 
     nothing = jnp.zeros((16, BLK), F32)
-    odd_coef_ref[...] = jnp.zeros_like(odd_coef_ref)
-    geometry(0, even_ref)
-    sums = lax.fori_loop(0, blocks // (2 * PAIR), trip, (nothing, nothing))
-    iso_sum, pull_sum = totals(blocks - PAIR, odd_coef_ref, sums)
+    iso_sum, pull_sum = lax.fori_loop(0, blocks // UNROLL, trip, (nothing, nothing))
     vel = ALPHA * (iso_sum[0:3] + iso_sum[3:6]) + BETA * (
         (hi + mid) * pull_sum[12:13] - (pull_sum[6:9] + pull_sum[9:12])
     )
@@ -170,10 +166,6 @@
         scratch_shapes=[
             pltpu.VMEM((2, blocks * KROWS, 128), F32),
             pltpu.VMEM((2, blocks * 16, 128), F32),
-            pltpu.VMEM((PAIR * BLK, 2 * BLK), F32),
-            pltpu.VMEM((PAIR * BLK, 2 * BLK), F32),
-            pltpu.VMEM((4, PAIR * BLK, BLK), BF),
-            pltpu.VMEM((4, PAIR * BLK, BLK), BF),
         ],
         cost_estimate=pl.CostEstimate(flops=10**8, bytes_accessed=10**6, transcendentals=0),
         compiler_params=pltpu.CompilerParams(vmem_limit_bytes=40 * 2**20),

time: 187 us -> 171 us (0.914)
  Pallas kernels: 64.8 us -> 48.6 us
    pallas_call x6, Pallas kernels: 64.8 us -> 48.6 us  [pair_step(): pl.pallas_call(lambda *refs: pair_kernel(blocks, *refs), out_shape=(out,...]
where the time goes in v2:
time: 171 us; the launch traced here: 170 us
  blocking collectives  82.5 us (48%)
  Pallas kernels  48.6 us (28%)
  waiting for transfers between devices  20.8 us (12%)
  starting transfers between devices  12.9 us (8%)
  local copies, waits for them, and re-layouts  3.13 us (2%)
    all_to_all x6, blocking collectives, sent_to_all(): return lax.all_to_all(copies, axis, split_axis=0, concat_axis=0, tiled=True)  82.5 us
    pallas_call x6, Pallas kernels, pair_step(): pl.pallas_call(lambda *refs: pair_kernel(blocks, *refs), out_shape=(out,...  48.6 us
    all_to_all x1, waiting for transfers between devices, sent_to_all(): return lax.all_to_all(copies, axis, split_axis=0, concat_axis=0, tiled=True)  20.8 us
    all_to_all x1, starting transfers between devices, sent_to_all(): return lax.all_to_all(copies, axis, split_axis=0, concat_axis=0, tiled=True)  12.9 us
  transfers between devices with their start and end apart: 1, of which 1 were waited for; matrix products, arithmetic and copies ran while one was open for 0% of the time, Pallas kernels for 0%

profile of v2, /device:TPU:1, one launch (start us, length us, event | category | flops | bytes accessed | tf_op | source)
XLA Modules:
  0.0 170.3 jit_solution(4920925642210272323)
XLA Ops:
  0.6 0.0 copy-start
  0.6 0.8 reshape.65
  1.4 0.0 copy-done
  1.4 1.2 broadcast_in_dim.36
  2.6 0.0 copy-start.3
  2.6 12.9 %all-to-all-start = ((f32[32,1,5376]{2,1,0:T(1,128)}), f32[32,1,5376]{2,1,0:T(1,128)S(1)}, u32[]{:S(2)}, u32[]{:S(2)}) async-start(f32[32,1,5376]{2,1,0:T(1,128)} %broadcast_in_dim.36), calls=%async_computation | async-start | bytes 1376256 | tf_op jit(solution)/shard_map/all_to_all | solution.py:178
  15.5 0.0 copy-done.3
  15.5 20.8 %all-to-all-done = f32[32,1,5376]{2,1,0:T(1,128)S(1)} async-done(((f32[32,1,5376]{2,1,0:T(1,128)}), f32[32,1,5376]{2,1,0:T(1,128)S(1)}, u32[]{:S(2)}, u32[]{:S(2)}) %all-to-all-start) | async-done | bytes 688160 | tf_op jit(solution)/shard_map/all_to_all | solution.py:178
  36.4 0.1 fusion.5
  36.5 8.1 %pair_step.6 = (f32[3,256]{1,0:T(4,128)S(1)}, f32[3,256]{1,0:T(4,128)}) custom-call(f32[32,768]{1,0:T(8,128)S(1)} %get-tuple-element.23.refs_0_, f32[32,768]{1,0:T(8,128)S(1)} %get-tuple-element.22.refs_1_, f32[3,256]{1,0:T(4,128)S(1)} %copy-done, f32[3,256]{1,0:T(4,128)S(1)} %get-tuple-element.28.refs_3_), custom_call_target="tpu_custom_call" | custom-call | flops 100000000 | bytes 1000000 | tf_op jit(solution)/shard_map/pair_step/pallas_call | solution.py:161
  44.6 0.1 broadcast_in_dim.38
  44.6 15.5 %all_to_all.55 = f32[32,1,768]{2,1,0:T(1,128)S(1)} all-to-all(f32[32,1,768]{2,1,0:T(1,128)S(1)} %broadcast_in_dim.38), channel_id=1, replica_groups=mesh['rep'=8,'blk'=32] {'blk'}, dimensions={0} | all-to-all | bytes 196608 | tf_op jit(solution)/shard_map/all_to_all | solution.py:178
  60.1 8.1 %pair_step.7 = (f32[3,256]{1,0:T(4,128)S(1)}, f32[3,256]{1,0:T(4,128)}) custom-call(f32[32,768]{1,0:T(8,128)S(1)} %bitcast.35, f32[32,768]{1,0:T(8,128)S(1)} %get-tuple-element.21.refs_1_, f32[3,256]{1,0:T(4,128)S(1)} %get-tuple-element.10.refs_2_, f32[3,256]{1,0:T(4,128)S(1)} %get-tuple-element.27.refs_3_), custom_call_target="tpu_custom_call" | custom-call | flops 100000000 | bytes 1000000 | tf_op jit(solution)/shard_map/pair_step/pallas_call | solution.py:161
  68.2 0.1 broadcast_in_dim.40
  68.3 13.5 %all_to_all.56 = f32[32,1,768]{2,1,0:T(1,128)S(1)} all-to-all(f32[32,1,768]{2,1,0:T(1,128)S(1)} %broadcast_in_dim.40), channel_id=1, replica_groups=mesh['rep'=8,'blk'=32] {'blk'}, dimensions={0} | all-to-all | bytes 196608 | tf_op jit(solution)/shard_map/all_to_all | solution.py:178
  81.8 8.1 %pair_step.8 = (f32[3,256]{1,0:T(4,128)S(1)}, f32[3,256]{1,0:T(4,128)}) custom-call(f32[32,768]{1,0:T(8,128)S(1)} %bitcast.36, f32[32,768]{1,0:T(8,128)S(1)} %get-tuple-element.20.refs_1_, f32[3,256]{1,0:T(4,128)S(1)} %get-tuple-element.11.refs_2_, f32[3,256]{1,0:T(4,128)S(1)} %get-tuple-element.26.refs_3_), custom_call_target="tpu_custom_call" | custom-call | flops 100000000 | bytes 1000000 | tf_op jit(solution)/shard_map/pair_step/pallas_call | solution.py:161
  89.9 0.1 broadcast_in_dim.42
  90.0 13.5 %all_to_all.57 = f32[32,1,768]{2,1,0:T(1,128)S(1)} all-to-all(f32[32,1,768]{2,1,0:T(1,128)S(1)} %broadcast_in_dim.42), channel_id=1, replica_groups=mesh['rep'=8,'blk'=32] {'blk'}, dimensions={0} | all-to-all | bytes 196608 | tf_op jit(solution)/shard_map/all_to_all | solution.py:178
  103.5 8.1 %pair_step.9 = (f32[3,256]{1,0:T(4,128)S(1)}, f32[3,256]{1,0:T(4,128)}) custom-call(f32[32,768]{1,0:T(8,128)S(1)} %bitcast.37, f32[32,768]{1,0:T(8,128)S(1)} %get-tuple-element.19.refs_1_, f32[3,256]{1,0:T(4,128)S(1)} %get-tuple-element.12.refs_2_, f32[3,256]{1,0:T(4,128)S(1)} %get-tuple-element.25.refs_3_), custom_call_target="tpu_custom_call" | custom-call | flops 100000000 | bytes 1000000 | tf_op jit(solution)/shard_map/pair_step/pallas_call | solution.py:161
  111.6 0.1 broadcast_in_dim.44
  111.6 13.5 %all_to_all.58 = f32[32,1,768]{2,1,0:T(1,128)S(1)} all-to-all(f32[32,1,768]{2,1,0:T(1,128)S(1)} %broadcast_in_dim.44), channel_id=1, replica_groups=mesh['rep'=8,'blk'=32] {'blk'}, dimensions={0} | all-to-all | bytes 196608 | tf_op jit(solution)/shard_map/all_to_all | solution.py:178
  125.1 8.1 %pair_step.10 = (f32[3,256]{1,0:T(4,128)S(1)}, f32[3,256]{1,0:T(4,128)}) custom-call(f32[32,768]{1,0:T(8,128)S(1)} %bitcast.38, f32[32,768]{1,0:T(8,128)S(1)} %get-tuple-element.18.refs_1_, f32[3,256]{1,0:T(4,128)S(1)} %get-tuple-element.13.refs_2_, f32[3,256]{1,0:T(4,128)S(1)} %get-tuple-element.29.refs_3_), custom_call_target="tpu_custom_call" | custom-call | flops 100000000 | bytes 1000000 | tf_op jit(solution)/shard_map/pair_step/pallas_call | solution.py:161
  133.2 0.0 copy-start.2
  133.2 0.1 broadcast_in_dim.46
  133.3 0.0 copy-start.1
  133.3 13.6 %all_to_all.59 = f32[32,1,768]{2,1,0:T(1,128)S(1)} all-to-all(f32[32,1,768]{2,1,0:T(1,128)S(1)} %broadcast_in_dim.46), channel_id=1, replica_groups=mesh['rep'=8,'blk'=32] {'blk'}, dimensions={0} | all-to-all | bytes 196608 | tf_op jit(solution)/shard_map/all_to_all | solution.py:178
  147.0 8.1 %pair_step.11 = (f32[3,256]{1,0:T(4,128)}, f32[3,256]{1,0:T(4,128)}) custom-call(f32[32,768]{1,0:T(8,128)S(1)} %bitcast.34, f32[32,768]{1,0:T(8,128)S(1)} %get-tuple-element.17.refs_1_, f32[3,256]{1,0:T(4,128)S(1)} %get-tuple-element.14.refs_2_, f32[3,256]{1,0:T(4,128)S(1)} %get-tuple-element.24.refs_3_), custom_call_target="tpu_custom_call" | custom-call | flops 100000000 | bytes 1000000 | tf_op jit(solution)/shard_map/pair_step/pallas_call | solution.py:161
  155.0 0.0 copy-start.4
  155.0 0.7 sub.12
  155.7 0.0 copy-done.2
  155.7 0.0 copy-done.1
  155.7 0.0 copy-done.4
  155.7 0.1 multiply_reduce_fusion
  155.9 12.8 %all_to_all.60 = f32[32,1,256]{2,1,0:T(1,128)S(1)} all-to-all(f32[32,1,256]{2,1,0:T(1,128)S(1)} %broadcast_in_dim.47), channel_id=1, replica_groups=mesh['rep'=8,'blk'=32] {'blk'}, dimensions={0} | all-to-all | bytes 65536 | tf_op jit(solution)/shard_map/all_to_all | solution.py:178
  168.8 0.1 reduce_sum.29
  168.8 0.0 copy-start.5
  168.8 0.6 copy-done.5
  169.5 0.8 convolution_multiply_fusion
  (17 shorter events, 0.2 us)
Async XLA Ops:
  0.6 0.8 copy-start
  2.6 12.9 %copy-start.3 = (f32[6,3,256]{2,1,0:T(4,128)S(1)}, f32[6,3,256]{2,1,0:T(4,128)}, u32[]{:S(2)}) copy-start(f32[6,3,256]{2,1,0:T(4,128)} %param.8) | copy-start | bytes 55300
  2.6 33.7 %all-to-all-start = ((f32[32,1,5376]{2,1,0:T(1,128)}), f32[32,1,5376]{2,1,0:T(1,128)S(1)}, u32[]{:S(2)}, u32[]{:S(2)}) async-start(f32[32,1,5376]{2,1,0:T(1,128)} %broadcast_in_dim.36), calls=%async_computation | async-start | bytes 1376256 | tf_op jit(solution)/shard_map/all_to_all | solution.py:178
  133.2 22.5 %copy-start.2 = (f32[128,3,256]{2,0,1:T(8,128)S(1)}, f32[128,3,256]{2,0,1:T(8,128)}, u32[]{:S(2)}) copy-start(f32[128,3,256]{2,0,1:T(8,128)} %param.9) | copy-start | bytes 1179652
  133.3 22.4 %copy-start.1 = (f32[128,3,256]{2,0,1:T(8,128)S(1)}, f32[128,3,256]{2,0,1:T(8,128)}, u32[]{:S(2)}) copy-start(f32[128,3,256]{2,0,1:T(8,128)} %param.10) | copy-start | bytes 1179652
  155.0 0.7 copy-start.4
  168.8 0.7 copy-start.5
